TPU v7x, 32 devices: a whole 2x2x4 slice. The times are simulated.
32 devices in a mesh: train: 4 (over y, x), induce: 8 (over z, core).
Axes of the slice: x: 2, y: 2, z: 4, core: 2. Of those that a mesh axis runs over, the one named last changes fastest.
Arguments:
- train_coords: float32 [256, 192], P('train'), may hold values from -0.3 to 4.8, as said below
- induce_coords: float32 [1024, 192], P('induce'), may hold values from -0.3 to 4.8, as said below
- train_forces: float32 [256, 192], P('train'), may hold values from -18 to 18
- atom_pairs: int32 [2, 2016], replicated, may hold values from 0 to 63, as said below
- length_scale: float32 [1], replicated, may hold values from 1.5 to 3
Outputs:
- coefficients: float32 [1024, 192], P('induce')
- residual: float32 [1024, 192], P('induce')
- desc_coeffs: float32 [1024, 2016], P('induce')
Inputs may be any that keep to these rules, and one draw needn't show every extreme that they name: `atom_pairs`: every unordered pair of two different atoms of the 64 stands in exactly one column, in either order. `train_coords`: atom a lies within 0.3 of 1.5 * (a % 4, a // 4 % 4, a // 16) in each component. `induce_coords`: atom a lies within 0.3 of 1.5 * (a % 4, a // 4 % 4, a // 16) in each component.
All inputs are finite; a program needn't handle non-finite values.
Results may differ from a plain program's by a relative error of at most 0.0085.
Values sent between devices are 32-bit elements; how exact they have to be, the bound alone decides.
No kernel may reach another device: no remote copies, remote signals or barrier semaphores. Data moves between devices by JAX's collectives and lax.ppermute only.
A program may use at most 64 MiB of HBM per device.

v0:
```python
import math
import jax
import jax.numpy as jnp
from jax import lax
from jax.sharding import PartitionSpec as P

root_five = math.sqrt(5.0)


def make_incidence(atom_pairs, atom_count):
    atom_ids = jnp.arange(atom_count, dtype=jnp.int32)
    head_hit = (atom_pairs[0][:, None] == atom_ids[None, :]).astype(jnp.float32)
    tail_hit = (atom_pairs[1][:, None] == atom_ids[None, :]).astype(jnp.float32)
    return head_hit - tail_hit


def lattice_coords(atom_count):
    atom_ids = jnp.arange(atom_count, dtype=jnp.int32)
    lattice = jnp.stack([atom_ids % 4, atom_ids // 4 % 4, atom_ids // 16]).astype(jnp.float32)
    return (1.5 * lattice).reshape(1, 3 * atom_count)


def describe(coords, incidence):
    atom_count = incidence.shape[1]
    spatial = coords.reshape(coords.shape[0], 3, atom_count)
    offsets = jnp.einsum("bca,pa->bcp", spatial, incidence, precision=lax.Precision.HIGHEST)
    length = jnp.sqrt(jnp.sum(offsets * offsets, axis=1))
    return (1.0 / length, offsets / (length**3)[:, None, :])


def centered(coords, incidence):
    values, gradients = describe(coords, incidence)
    lattice_values = describe(lattice_coords(incidence.shape[1]), incidence)[0]
    return ((values - lattice_values).astype(jnp.bfloat16), gradients)


def to_desc(gradients, vectors, incidence):
    atom_count = incidence.shape[1]
    shifted = jnp.einsum(
        "bca,pa->bcp",
        vectors.reshape(vectors.shape[0], 3, atom_count),
        incidence,
        precision=lax.Precision.HIGHEST,
    )
    return -jnp.sum(gradients * shifted, axis=1)


def to_forces(gradients, values, incidence):
    weighted = gradients * values[:, None, :]
    summed = jnp.einsum("bcp,pa->bca", weighted, incidence, precision=lax.Precision.HIGHEST)
    return -summed.reshape(values.shape[0], -1)


def matern(row_desc, col_desc, length):
    inner_prod = jnp.dot(row_desc, col_desc.T, preferred_element_type=jnp.float32)
    row_sq = jnp.sum(jnp.square(row_desc.astype(jnp.float32)), axis=1)
    col_sq = jnp.sum(jnp.square(col_desc.astype(jnp.float32)), axis=1)
    radius = jnp.sqrt(row_sq[:, None] + col_sq[None, :] - 2.0 * inner_prod) / length
    falloff = jnp.exp(-root_five * radius)
    diag_part = 5.0 / (3.0 * length**2) * (1.0 + root_five * radius) * falloff
    outer_part = 25.0 / (3.0 * length**4) * falloff
    return (diag_part, outer_part)


def apply_forward(train_desc, induce_desc, diag_part, outer_part, induce_vals):
    self_dot = jnp.sum(induce_desc.astype(jnp.float32) * induce_vals.astype(jnp.float32), axis=1)
    projected = (
        jnp.dot(train_desc, induce_vals.T, preferred_element_type=jnp.float32) - self_dot[None, :]
    )
    product = outer_part * projected
    result = jnp.dot(
        diag_part.astype(jnp.bfloat16), induce_vals, preferred_element_type=jnp.float32
    )
    result = result + jnp.dot(
        product.astype(jnp.bfloat16), induce_desc, preferred_element_type=jnp.float32
    )
    return result - train_desc.astype(jnp.float32) * jnp.sum(product, axis=1)[:, None]


def apply_adjoint(train_desc, induce_desc, diag_part, outer_part, train_vals):
    self_dot = jnp.sum(train_desc.astype(jnp.float32) * train_vals.astype(jnp.float32), axis=1)
    projected = self_dot[:, None] - jnp.dot(
        train_vals, induce_desc.T, preferred_element_type=jnp.float32
    )
    product = outer_part * projected
    result = jnp.dot(
        diag_part.astype(jnp.bfloat16).T, train_vals, preferred_element_type=jnp.float32
    )
    result = result - jnp.dot(
        product.astype(jnp.bfloat16).T, train_desc, preferred_element_type=jnp.float32
    )
    return result + induce_desc.astype(jnp.float32) * jnp.sum(product, axis=0)[:, None]


def per_device(train_coords, induce_coords, train_forces, atom_pairs, length_scale):
    atom_count = train_coords.shape[1] // 3
    incidence = make_incidence(atom_pairs, atom_count)
    train_desc, train_grad = centered(train_coords, incidence)
    induce_desc, induce_grad = centered(induce_coords, incidence)
    diag_part, outer_part = matern(train_desc, induce_desc, length_scale[0])

    def forward(vectors):
        vectors = lax.all_gather(vectors, "train", axis=0, tiled=True)
        induce_vals = to_desc(induce_grad, vectors, incidence).astype(jnp.bfloat16)
        partial_forces = to_forces(
            train_grad,
            apply_forward(train_desc, induce_desc, diag_part, outer_part, induce_vals),
            incidence,
        )
        return lax.psum(partial_forces, "induce")

    def adjoint(forces_like):
        train_vals = to_desc(train_grad, forces_like, incidence).astype(jnp.bfloat16)
        partial_coeffs = to_forces(
            induce_grad,
            apply_adjoint(train_desc, induce_desc, diag_part, outer_part, train_vals),
            incidence,
        )
        return lax.psum_scatter(partial_coeffs, "train", scatter_dimension=0, tiled=True)

    start = adjoint(train_forces)
    probed = forward(start)
    probed_local = jnp.sum(probed * probed)
    cross_local = jnp.sum(train_forces * probed)
    probed_sq = lax.psum(probed_local, "train")
    cross_sq = lax.psum(cross_local, "train")
    quotient = probed_sq / cross_sq
    center = 0.775 * quotient
    spread = 0.725 * quotient
    momentum = spread / center
    direction = start / center
    coefficients = direction
    residual = start - adjoint(probed) / center
    momentum_next = 1.0 / (2.0 * center / spread - momentum)
    direction = momentum_next * momentum * direction + 2.0 * momentum_next / spread * residual
    coefficients = coefficients + direction
    residual = residual - adjoint(forward(direction))
    coefficients, residual = (
        lax.all_gather(coefficients, "train", axis=0, tiled=True),
        lax.all_gather(residual, "train", axis=0, tiled=True),
    )
    desc_coeffs = to_desc(induce_grad, coefficients, incidence)
    return (coefficients, residual, desc_coeffs)


def solution(mesh):
    in_specs = (P("train", None), P("induce", None), P("train", None), P(), P())
    out_specs = (P("induce", None), P("induce", None), P("induce", None))
    return jax.shard_map(
        per_device, mesh=mesh, in_specs=in_specs, out_specs=out_specs, check_vma=False
    )
```

profile of v0, /device:TPU:0, one launch (start us, length us, event | category | flops | bytes accessed | tf_op | source)
XLA Modules:
  0.0 235.9 jit_solution(11568177319664420499)
XLA Ops:
  7.9 0.8 fusion.121
  8.7 0.5 fusion.46
  9.2 0.9 copy.35
  10.2 1.0 copy.33
  11.1 1.5 multiply_reduce_fusion.3
  12.8 4.5 %fusion = (f32[128,2016]{0,1:T(8,128)S(1)}, f32[2016,128,3]{1,0,2:T(8,128)}) fusion(f32[128,3,64]{0,2,1:T(8,128)S(1)} %bitcast.109, s32[2016]{0:T(1024)S(1)} %bitcast.136, s32[2016]{0:T(1024)S(1)} %bitcast.122), kind=kOutput, calls=%fused_computation.2 | convolution fusion | flops 596477952 | bytes 4243200 | tf_op jit(solution)/shard_map/bca,pa->bcp/dot_general | solution.py:26
  17.4 1.6 fusion.20
  19.3 0.5 fusion.47
  20.0 0.4 fusion.116
  20.7 0.4 fusion.10
  21.1 1.2 copy-done.1
  22.3 2.3 fusion.29
  24.6 0.8 copy.53
  25.4 27.0 %reduce-scatter.10.cloned.1.call-done = f32[32,192]{1,0:T(8,128)} async-done(((f32[128,192]{1,0:T(8,128)}), f32[32,192]{1,0:T(8,128)}) %reduce-scatter.10.cloned.1.call-update) | async-done | bytes 24592 | tf_op jit(solution)/shard_map/reduce_scatter | solution.py:119
  52.4 8.6 %all_gather.12 = f32[128,192]{1,0:T(8,128)S(1)} all-gather(f32[32,192]{1,0:T(8,128)} %reduce-scatter.10.cloned.1.call-done), channel_id=1, replica_groups=mesh['train'=4,'induce'=8] {'train'}, dimensions={0}, use_global_device_ids=true | all-gather | bytes 122880 | tf_op jit(solution)/shard_map/all_gather | solution.py:103
  61.1 5.3 %multiply_reduce_fusion.2 = f32[128,2016]{0,1:T(8,128)S(1)} fusion(f32[128,3,64]{0,2,1:T(8,128)S(1)} %bitcast.116, s32[2016]{0:T(1024)S(1)} %bitcast.139, s32[2016]{0:T(1024)S(1)} %bitcast.125, f32[128,2016]{0,1:T(8,128)S(1)} %get-tuple-element.20, f32[2016,128,3]{1,0,2:T(8,128)} %get-tuple-element.26), kind=kOutput, calls=%fused_computation.9 | convolution fusion | flops 597252096 | bytes 5275392 | tf_op jit(solution)/shard_map/bca,pa->bcp/dot_general | solution.py:39
  67.9 2.2 fusion.23
  70.1 1.6 copy.39
  71.7 28.0 %psum.28 = f32[64,192]{0,1:T(8,128)} all-reduce(f32[64,192]{0,1:T(8,128)} %bitcast.113), channel_id=1, replica_groups=mesh['train'=4,'induce'=8] {'induce'}, use_global_device_ids=true, to_apply=%region_12.13 | all-reduce | flops 12288 | bytes 98304 | tf_op jit(solution)/shard_map/psum | solution.py:110
  99.7 2.8 %fusion.21 = f32[64,2016]{1,0:T(8,128)S(1)} fusion(f32[64,3,64]{0,2,1:T(8,128)} %bitcast.112, s32[2016]{0:T(1024)S(1)} %bitcast.141, s32[2016]{0:T(1024)S(1)} %bitcast.127, f32[64,3,2016]{2,0,1:T(8,128)S(1)} %copy-done.5, f32[64,2016]{1,0:T(8,128)} %copy-done.6), kind=kOutput, calls=%fused_computation.44 | convolution fusion | flops 298948608 | bytes 2645760 | tf_op jit(solution)/shard_map/bca,pa->bcp/dot_general | solution.py:39
  102.7 0.4 fusion.117
  103.4 0.4 fusion.9
  103.8 0.6 copy-done.2
  104.4 2.9 %fusion.32 = f32[128,3,64]{0,2,1:T(8,128)} fusion(f32[128,2016]{0,1:T(8,128)S(1)} %fusion.9, s32[2016]{0:T(1024)S(1)} %bitcast.142, s32[2016]{0:T(1024)S(1)} %bitcast.128, f32[2016,128,3]{1,0,2:T(8,128)S(1)} %copy-done.2, f32[128,2016]{0,1:T(8,128)S(1)} %get-tuple-element.20), kind=kOutput, calls=%fused_computation.55 | convolution fusion | flops 596760576 | bytes 5275392 | tf_op jit(solution)/shard_map/bcp,pa->bca/dot_general | solution.py:50
  107.3 1.6 copy.55
  109.0 1.6 multiply_reduce_fusion.4
  110.7 9.5 %all-reduce = (f32[]{:T(128)}, f32[]{:T(128)}) all-reduce(f32[]{:T(128)} %get-tuple-element.12, f32[]{:T(128)} %get-tuple-element.11), channel_id=1, replica_groups=mesh['train'=4,'induce'=8] {'train'}, use_global_device_ids=true, to_apply=%region_14.15 | all-reduce | flops 2 | bytes 16 | tf_op jit(solution)/shard_map/psum | solution.py:125
  121.7 8.8 %reduce-scatter.12.cloned.1.call-done = f32[32,192]{1,0:T(8,128)} async-done(((f32[128,192]{1,0:T(8,128)}), f32[32,192]{1,0:T(8,128)}) %reduce-scatter.12.cloned.1.call-update) | async-done | bytes 24592 | tf_op jit(solution)/shard_map/reduce_scatter | solution.py:119
  130.5 1.4 fusion.104
  131.9 9.3 %all_gather.14 = f32[128,192]{1,0:T(8,128)} all-gather(f32[32,192]{1,0:T(8,128)S(1)} %get-tuple-element.16), channel_id=1, replica_groups=mesh['train'=4,'induce'=8] {'train'}, dimensions={0}, use_global_device_ids=true | all-gather | bytes 122880 | tf_op jit(solution)/shard_map/all_gather | solution.py:103
  141.2 1.6 copy.45
  142.8 5.3 %multiply_reduce_fusion.1 = f32[128,2016]{0,1:T(8,128)S(1)} fusion(f32[128,3,64]{0,2,1:T(8,128)} %bitcast.118, s32[2016]{0:T(1024)S(1)} %bitcast.143, s32[2016]{0:T(1024)S(1)} %bitcast.129, f32[128,2016]{0,1:T(8,128)S(1)} %get-tuple-element.20, f32[2016,128,3]{1,0,2:T(8,128)} %get-tuple-element.26), kind=kOutput, calls=%fused_computation.6 | convolution fusion | flops 597252096 | bytes 5275392 | tf_op jit(solution)/shard_map/bca,pa->bcp/dot_general | solution.py:39
  149.5 2.2 fusion.26
  151.6 27.5 %psum.31 = f32[64,3,64]{2,0,1:T(8,128)S(1)} all-reduce(f32[64,3,64]{2,0,1:T(8,128)} %fusion.26), channel_id=1, replica_groups=mesh['train'=4,'induce'=8] {'induce'}, use_global_device_ids=true, to_apply=%region_24.25 | all-reduce | flops 12288 | bytes 98304 | tf_op jit(solution)/shard_map/psum | solution.py:110
  179.1 3.1 %fusion.22 = f32[64,2016]{1,0:T(8,128)S(1)} fusion(f32[64,3,64]{2,0,1:T(8,128)S(1)} %psum.31, s32[2016]{0:T(1024)S(1)} %bitcast.145, s32[2016]{0:T(1024)S(1)} %bitcast.131, f32[64,3,2016]{2,0,1:T(8,128)} %copy-done.4, f32[64,2016]{1,0:T(8,128)} %copy-done.6), kind=kOutput, calls=%fused_computation.45 | convolution fusion | flops 298948608 | bytes 2645760 | tf_op jit(solution)/shard_map/bca,pa->bcp/dot_general | solution.py:39
  182.4 0.4 fusion.118
  182.8 8.5 %all_gather.13 = f32[128,192]{1,0:T(8,128)} all-gather(f32[32,192]{1,0:T(8,128)S(1)} %copy-done.11), channel_id=1, replica_groups=mesh['train'=4,'induce'=8] {'train'}, dimensions={0}, use_global_device_ids=true | all-gather | bytes 122880 | tf_op jit(solution)/shard_map/all_gather | solution.py:139
  191.2 1.6 copy.48
  193.1 0.4 fusion.8
  193.5 1.2 copy-done.3
  194.8 2.3 fusion.35
  197.0 0.8 copy.57
  197.8 5.3 %multiply_reduce_fusion = f32[128,2016]{0,1:T(8,128)S(1)} fusion(f32[128,3,64]{0,2,1:T(8,128)S(1)} %bitcast.114, s32[2016]{0:T(1024)S(1)} %bitcast.147, s32[2016]{0:T(1024)S(1)} %bitcast.133, f32[128,2016]{0,1:T(8,128)S(1)} %get-tuple-element.20, f32[2016,128,3]{1,0,2:T(8,128)} %get-tuple-element.26), kind=kOutput, calls=%fused_computation.3 | convolution fusion | flops 597252096 | bytes 5275392 | tf_op jit(solution)/shard_map/bca,pa->bcp/dot_general | solution.py:39
  203.1 1.0 neg.63
  204.2 15.2 %reduce-scatter.14.cloned.1.call-done = f32[32,192]{1,0:T(8,128)} async-done(((f32[128,192]{1,0:T(8,128)}), f32[32,192]{1,0:T(8,128)}) %reduce-scatter.14.cloned.1.call-update) | async-done | bytes 24592 | tf_op jit(solution)/shard_map/reduce_scatter | solution.py:119
  219.3 0.8 fusion.115
  220.1 8.5 %all_gather.15 = f32[128,192]{1,0:T(8,128)S(1)} all-gather(f32[32,192]{1,0:T(8,128)S(1)} %fusion.115), channel_id=1, replica_groups=mesh['train'=4,'induce'=8] {'train'}, dimensions={0}, use_global_device_ids=true | all-gather | bytes 122880 | tf_op jit(solution)/shard_map/all_gather | solution.py:140
  228.6 0.7 copy.49
  (51 shorter events, 5.0 us)
Async XLA Ops:
  7.2 5.7 %copy-start = (f32[128,192]{0,1:T(8,128)S(1)}, f32[128,192]{0,1:T(8,128)}, u32[]{:S(2)}) copy-start(f32[128,192]{0,1:T(8,128)} %param.6) | copy-start | bytes 294916
  7.2 45.2 %reduce-scatter.10.cloned.1.call-start = ((), (), s32[]{:S(2)}) async-start(), calls=%async_computation.3 | async-start | bytes 163840 | tf_op jit(solution)/shard_map/reduce_scatter | solution.py:119
  10.2 7.2 %copy-start.9 = (f32[64,192]{0,1:T(8,128)}, f32[64,192]{0,1:T(8,128)S(1)}, u32[]{:S(2)}) copy-start(f32[64,192]{0,1:T(8,128)S(1)} %copy.35) | copy-start | bytes 147460
  12.6 6.3 %copy-start.4 = (f32[64,3,2016]{2,0,1:T(8,128)}, f32[64,3,2016]{2,0,1:T(8,128)S(1)}, u32[]{:S(2)}) copy-start(f32[64,3,2016]{2,0,1:T(8,128)S(1)} %get-tuple-element.24) | copy-start | bytes 4644868
  12.8 6.2 %copy-start.6 = (f32[64,2016]{1,0:T(8,128)}, f32[64,2016]{1,0:T(8,128)S(1)}, u32[]{:S(2)}) copy-start(f32[64,2016]{1,0:T(8,128)S(1)} %multiply_multiply_fusion.1) | copy-start | bytes 1548292
  20.5 1.9 copy-start.1
  25.4 105.1 %reduce-scatter.12.cloned.1.call-start = ((), (), s32[]{:S(2)}) async-start(), calls=%async_computation.4 | async-start | bytes 163840 | tf_op jit(solution)/shard_map/reduce_scatter | solution.py:119
  66.4 1.4 copy-start.5
  66.4 1.5 copy-start.7
  102.5 1.9 copy-start.2
  109.0 110.4 %reduce-scatter.14.cloned.1.call-start = ((), (), s32[]{:S(2)}) async-start(), calls=%async_computation.5 | async-start | bytes 163840 | tf_op jit(solution)/shard_map/reduce_scatter | solution.py:119
  148.1 1.3 copy-start.8
  179.1 3.7 %copy-start.11 = (f32[32,192]{1,0:T(8,128)S(1)}, f32[32,192]{1,0:T(8,128)}, u32[]{:S(2)}) copy-start(f32[32,192]{1,0:T(8,128)} %get-tuple-element.15) | copy-start | bytes 73732
  192.9 1.9 copy-start.3
  194.7 3.0 %copy-start.13 = (f32[128,192]{0,1:T(8,128)S(1)}, f32[128,192]{0,1:T(8,128)}, u32[]{:S(2)}) copy-start(f32[128,192]{0,1:T(8,128)} %copy.48) | copy-start | bytes 294916
  197.8 21.5 %copy-start.10 = (f32[32,192]{1,0:T(8,128)S(1)}, f32[32,192]{1,0:T(8,128)}, u32[]{:S(2)}) copy-start(f32[32,192]{1,0:T(8,128)} %reduce-scatter.10.cloned.1.call-done) | copy-start | bytes 73732
  197.8 21.5 %copy-start.12 = (f32[32,192]{1,0:T(8,128)S(1)}, f32[32,192]{1,0:T(8,128)}, u32[]{:S(2)}) copy-start(f32[32,192]{1,0:T(8,128)} %reduce-scatter.12.cloned.1.call-done) | copy-start | bytes 73732
Sparse Core Ops, SparseCore 0:
  25.5 26.8 reduce-scatter.9
  109.1 21.3 reduce-scatter.11
  197.9 21.3 reduce-scatter.13
where the time goes:
time: 237 us; the launch traced here: 236 us
  blocking collectives  99.8 us (42%)
  waiting for transfers between devices  51 us (22%)
  matrix products  46.9 us (20%)
  between operations  16.3 us (7%)
  local copies, waits for them, and re-layouts  15 us (6%)
  other arithmetic  6.73 us (3%)
    psum x2, blocking collectives, forward(): return lax.psum(partial_forces, 'induce')  55.5 us
    reduce_scatter x3, waiting for transfers between devices, adjoint(): lax.psum_scatter(partial_coeffs, 'train', scatter_dimension=0, tiled=True)  51 us
    dot_general x6, matrix products, to_desc(): jnp.einsum('bca,pa->bcp', vectors.reshape(vectors.shape[0], 3, atom_count...  23.4 us
    all_gather x2, blocking collectives, forward(): vectors = lax.all_gather(vectors, 'train', axis=0, tiled=True)  17.8 us
    dot_general x5, matrix products, to_forces(): jnp.einsum('bcp,pa->bca', weighted, incidence, precision=lax.Precision.HI...  11.7 us
    unnamed x35, local copies, waits for them, and re-layouts  10.8 us
    psum x1, blocking collectives, per_device(): probed_sq = lax.psum(probed_local, 'train')  9.53 us
    all_gather x1, blocking collectives, per_device(): lax.all_gather(residual, 'train', axis=0, tiled=True)  8.46 us
  transfers between devices with their start and end apart: 3, of which 3 were waited for; matrix products, arithmetic and copies ran while one was open for 3% of the time, Pallas kernels for 0%

commit v1 on v0

--- a/solution.py
+++ b/solution.py
@@ -107,7 +107,7 @@
             apply_forward(train_desc, induce_desc, diag_part, outer_part, induce_vals),
             incidence,
         )
-        return lax.psum(partial_forces, "induce")
+        return jnp.sum(lax.all_gather(partial_forces, "induce"), axis=0)
 
     def adjoint(forces_like):
         train_vals = to_desc(train_grad, forces_like, incidence).astype(jnp.bfloat16)

time: 237 us -> 217 us (0.916)
  blocking collectives: 99.8 us -> 74.2 us
  waiting for transfers between devices: 51 us -> 56.4 us
    psum x2 -> x0, blocking collectives: 55.5 us -> none  [forward(): return lax.psum(partial_forces, 'induce')]
    all_gather x0 -> x2, blocking collectives: none -> 29.9 us  [forward(): return jnp.sum(lax.all_gather(partial_forces, 'induce'), axis=0)]
    reduce_scatter x3, waiting for transfers between devices: 51 us -> 56.3 us  [adjoint(): lax.psum_scatter(partial_coeffs, 'train', scatter_dimension=0, tiled=True)]
    unnamed x35 -> x39, local copies, waits for them, and re-layouts: 10.8 us -> 11.5 us
  transfers between devices with their start and end apart: 3 -> 3, of which waited for: 3 -> 3; matrix products, arithmetic and copies ran while one was open for 3% -> 4% of each run, Pallas kernels for 0% -> 0%
where the time goes in v1:
time: 217 us; the launch traced here: 216 us
  blocking collectives  74.2 us (34%)
  waiting for transfers between devices  56.4 us (26%)
  matrix products  46.4 us (21%)
  between operations  16.4 us (8%)
  local copies, waits for them, and re-layouts  15.5 us (7%)
  other arithmetic  6.73 us (3%)
    reduce_scatter x3, waiting for transfers between devices, adjoint(): lax.psum_scatter(partial_coeffs, 'train', scatter_dimension=0, tiled=True)  56.3 us
    all_gather x2, blocking collectives, forward(): return jnp.sum(lax.all_gather(partial_forces, 'induce'), axis=0)  29.9 us
    dot_general x6, matrix products, to_desc(): jnp.einsum('bca,pa->bcp', vectors.reshape(vectors.shape[0], 3, atom_count...  23.4 us
    all_gather x2, blocking collectives, forward(): vectors = lax.all_gather(vectors, 'train', axis=0, tiled=True)  17.8 us
    unnamed x39, local copies, waits for them, and re-layouts  11.5 us
    dot_general x5, matrix products, to_forces(): jnp.einsum('bcp,pa->bca', weighted, incidence, precision=lax.Precision.HI...  11.2 us
    psum x1, blocking collectives, per_device(): probed_sq = lax.psum(probed_local, 'train')  9.53 us
    all_gather x1, blocking collectives, per_device(): lax.all_gather(residual, 'train', axis=0, tiled=True)  8.47 us
  transfers between devices with their start and end apart: 3, of which 3 were waited for; matrix products, arithmetic and copies ran while one was open for 4% of the time, Pallas kernels for 0%

profile of v1, /device:TPU:0, one launch (start us, length us, event | category | flops | bytes accessed | tf_op | source)
XLA Modules:
  0.0 215.7 jit_solution(9409854702809433740)
XLA Ops:
  7.9 0.8 fusion.121
  8.7 0.5 fusion.46
  9.2 0.9 copy.61
  10.2 0.9 copy.63
  11.1 1.5 multiply_reduce_fusion.3
  12.8 4.5 %fusion = (f32[128,2016]{0,1:T(8,128)S(1)}, f32[2016,128,3]{1,0,2:T(8,128)}) fusion(f32[128,3,64]{0,2,1:T(8,128)S(1)} %bitcast.111, s32[2016]{0:T(1024)S(1)} %bitcast.140, s32[2016]{0:T(1024)S(1)} %bitcast.126), kind=kOutput, calls=%fused_computation.2 | convolution fusion | flops 596477952 | bytes 4243200 | tf_op jit(solution)/shard_map/bca,pa->bcp/dot_general | solution.py:26
  17.3 1.6 fusion.20
  19.2 0.5 fusion.47
  20.0 0.4 fusion.116
  20.7 0.4 fusion.10
  21.1 1.2 copy-done.1
  22.3 2.3 %fusion.29 = f32[128,3,64]{0,2,1:T(8,128)S(1)} fusion(f32[128,2016]{0,1:T(8,128)S(1)} %fusion.10, s32[2016]{0:T(1024)S(1)} %bitcast.142, s32[2016]{0:T(1024)S(1)} %bitcast.128, f32[2016,128,3]{1,0,2:T(8,128)S(1)} %copy-done.1, f32[128,2016]{0,1:T(8,128)S(1)} %get-tuple-element.23), kind=kOutput, calls=%fused_computation.54 | convolution fusion | flops 596760576 | bytes 5275392 | tf_op jit(solution)/shard_map/bcp,pa->bca/dot_general | solution.py:50
  24.6 0.8 copy.87
  25.4 27.0 %reduce-scatter.10.cloned.1.call-done = f32[32,192]{1,0:T(8,128)} async-done(((f32[128,192]{1,0:T(8,128)}), f32[32,192]{1,0:T(8,128)}) %reduce-scatter.10.cloned.1.call-update) | async-done | bytes 24592 | tf_op jit(solution)/shard_map/reduce_scatter | solution.py:119
  52.5 8.6 %all_gather.20 = f32[128,192]{1,0:T(8,128)S(1)} all-gather(f32[32,192]{1,0:T(8,128)} %reduce-scatter.10.cloned.1.call-done), channel_id=1, replica_groups=mesh['train'=4,'induce'=8] {'train'}, dimensions={0}, use_global_device_ids=true | all-gather | bytes 122880 | tf_op jit(solution)/shard_map/all_gather | solution.py:103
  61.1 5.3 %multiply_reduce_fusion.2 = f32[128,2016]{0,1:T(8,128)S(1)} fusion(f32[128,3,64]{0,2,1:T(8,128)S(1)} %bitcast.117, s32[2016]{0:T(1024)S(1)} %bitcast.143, s32[2016]{0:T(1024)S(1)} %bitcast.129, f32[128,2016]{0,1:T(8,128)S(1)} %get-tuple-element.23, f32[2016,128,3]{1,0,2:T(8,128)} %get-tuple-element.29), kind=kOutput, calls=%fused_computation.9 | convolution fusion | flops 597252096 | bytes 5275392 | tf_op jit(solution)/shard_map/bca,pa->bcp/dot_general | solution.py:39
  68.0 1.5 fusion.23
  69.7 15.0 %all_gather.21 = f32[8,64,192]{2,1,0:T(8,128)S(1)} all-gather(f32[1,64,192]{2,1,0:T(8,128)S(1)} %copy.68), channel_id=1, replica_groups=mesh['train'=4,'induce'=8] {'induce'}, dimensions={0}, use_global_device_ids=true | all-gather | bytes 442368 | tf_op jit(solution)/shard_map/all_gather | solution.py:110
  84.8 0.5 copy-done.8
  85.3 2.7 %fusion.21 = f32[64,2016]{1,0:T(8,128)S(1)} fusion(f32[64,3,64]{0,2,1:T(8,128)S(1)} %bitcast.123, s32[2016]{0:T(1024)S(1)} %bitcast.145, s32[2016]{0:T(1024)S(1)} %bitcast.131, f32[64,3,2016]{2,0,1:T(8,128)S(1)} %copy-done.5, f32[64,2016]{1,0:T(8,128)} %copy-done.9), kind=kOutput, calls=%fused_computation.44 | convolution fusion | flops 298948608 | bytes 2645760 | tf_op jit(solution)/shard_map/bca,pa->bcp/dot_general | solution.py:39
  88.9 0.4 fusion.9
  89.3 0.6 copy-done.2
  90.2 2.9 %fusion.32 = f32[128,3,64]{0,2,1:T(8,128)} fusion(f32[128,2016]{0,1:T(8,128)S(1)} %fusion.9, s32[2016]{0:T(1024)S(1)} %bitcast.146, s32[2016]{0:T(1024)S(1)} %bitcast.132, f32[2016,128,3]{1,0,2:T(8,128)S(1)} %copy-done.2, f32[128,2016]{0,1:T(8,128)S(1)} %copy-done.7), kind=kOutput, calls=%fused_computation.55 | convolution fusion | flops 596760576 | bytes 5275392 | tf_op jit(solution)/shard_map/bcp,pa->bca/dot_general | solution.py:50
  93.1 1.6 copy.89
  94.9 1.6 multiply_reduce_fusion.4
  96.4 9.5 %all-reduce = (f32[]{:T(128)}, f32[]{:T(128)}) all-reduce(f32[]{:T(128)} %get-tuple-element.15, f32[]{:T(128)} %get-tuple-element.14), channel_id=1, replica_groups=mesh['train'=4,'induce'=8] {'train'}, use_global_device_ids=true, to_apply=%region_14.15 | all-reduce | flops 2 | bytes 16 | tf_op jit(solution)/shard_map/psum | solution.py:125
  107.5 11.5 %reduce-scatter.12.cloned.1.call-done = f32[32,192]{1,0:T(8,128)} async-done(((f32[128,192]{1,0:T(8,128)}), f32[32,192]{1,0:T(8,128)}) %reduce-scatter.12.cloned.1.call-update) | async-done | bytes 24592 | tf_op jit(solution)/shard_map/reduce_scatter | solution.py:119
  119.0 1.4 fusion.104
  120.4 9.3 %all_gather.23 = f32[128,192]{1,0:T(8,128)} all-gather(f32[32,192]{1,0:T(8,128)S(1)} %get-tuple-element.19), channel_id=1, replica_groups=mesh['train'=4,'induce'=8] {'train'}, dimensions={0}, use_global_device_ids=true | all-gather | bytes 122880 | tf_op jit(solution)/shard_map/all_gather | solution.py:103
  129.6 1.6 copy.74
  131.3 5.3 %multiply_reduce_fusion.1 = f32[128,2016]{0,1:T(8,128)S(1)} fusion(f32[128,3,64]{0,2,1:T(8,128)} %bitcast.119, s32[2016]{0:T(1024)S(1)} %bitcast.147, s32[2016]{0:T(1024)S(1)} %bitcast.133, f32[128,2016]{0,1:T(8,128)S(1)} %copy-done.7, f32[2016,128,3]{1,0,2:T(8,128)} %get-tuple-element.29), kind=kOutput, calls=%fused_computation.6 | convolution fusion | flops 597252096 | bytes 5275392 | tf_op jit(solution)/shard_map/bca,pa->bcp/dot_general | solution.py:39
  137.9 2.2 %fusion.26 = f32[64,3,64]{2,0,1:T(8,128)} fusion(f32[64,2016]{1,0:T(8,128)S(1)} %fusion.11, s32[2016]{0:T(1024)S(1)} %bitcast.148, s32[2016]{0:T(1024)S(1)} %bitcast.134, f32[64,3,2016]{2,0,1:T(8,128)S(1)} %copy-done.5, f32[64,2016]{1,0:T(8,128)S(1)} %copy-done.11), kind=kOutput, calls=%fused_computation.53 | convolution fusion | flops 298702848 | bytes 2645760 | tf_op jit(solution)/shard_map/bcp,pa->bca/dot_general | solution.py:50
  140.1 1.0 copy.75
  141.2 15.0 %all_gather.24 = f32[8,64,192]{2,1,0:T(8,128)S(1)} all-gather(f32[1,64,192]{2,1,0:T(8,128)S(1)} %copy.76), channel_id=1, replica_groups=mesh['train'=4,'induce'=8] {'induce'}, dimensions={0}, use_global_device_ids=true | all-gather | bytes 442368 | tf_op jit(solution)/shard_map/all_gather | solution.py:110
  156.3 3.1 %fusion.22 = f32[64,2016]{1,0:T(8,128)S(1)} fusion(f32[64,3,64]{0,2,1:T(8,128)S(1)} %bitcast.122, s32[2016]{0:T(1024)S(1)} %bitcast.149, s32[2016]{0:T(1024)S(1)} %bitcast.135, f32[64,3,2016]{2,0,1:T(8,128)} %copy-done.4, f32[64,2016]{1,0:T(8,128)} %copy-done.9), kind=kOutput, calls=%fused_computation.45 | convolution fusion | flops 298948608 | bytes 2645760 | tf_op jit(solution)/shard_map/bca,pa->bcp/dot_general | solution.py:39
  159.6 0.4 fusion.118
  160.0 8.4 %all_gather.22 = f32[128,192]{1,0:T(8,128)} all-gather(f32[32,192]{1,0:T(8,128)S(1)} %copy-done.13), channel_id=1, replica_groups=mesh['train'=4,'induce'=8] {'train'}, dimensions={0}, use_global_device_ids=true | all-gather | bytes 122880 | tf_op jit(solution)/shard_map/all_gather | solution.py:139
  168.4 1.6 copy.81
  170.3 0.4 fusion.8
  170.7 1.2 copy-done.3
  172.0 2.3 %fusion.35 = f32[128,3,64]{0,2,1:T(8,128)S(1)} fusion(f32[128,2016]{0,1:T(8,128)S(1)} %fusion.8, s32[2016]{0:T(1024)S(1)} %bitcast.150, s32[2016]{0:T(1024)S(1)} %bitcast.136, f32[2016,128,3]{1,0,2:T(8,128)S(1)} %copy-done.3, f32[128,2016]{0,1:T(8,128)S(1)} %copy-done.7), kind=kOutput, calls=%fused_computation.56 | convolution fusion | flops 596760576 | bytes 5275392 | tf_op jit(solution)/shard_map/bcp,pa->bca/dot_general | solution.py:50
  174.2 0.8 copy.91
  175.1 5.3 %multiply_reduce_fusion = f32[128,2016]{0,1:T(8,128)S(1)} fusion(f32[128,3,64]{0,2,1:T(8,128)S(1)} %bitcast.115, s32[2016]{0:T(1024)S(1)} %bitcast.151, s32[2016]{0:T(1024)S(1)} %bitcast.137, f32[128,2016]{0,1:T(8,128)S(1)} %copy-done.7, f32[2016,128,3]{1,0,2:T(8,128)} %get-tuple-element.29), kind=kOutput, calls=%fused_computation.3 | convolution fusion | flops 597252096 | bytes 5275392 | tf_op jit(solution)/shard_map/bca,pa->bcp/dot_general | solution.py:39
  180.4 1.0 neg.77
  181.4 17.8 %reduce-scatter.14.cloned.1.call-done = f32[32,192]{1,0:T(8,128)} async-done(((f32[128,192]{1,0:T(8,128)}), f32[32,192]{1,0:T(8,128)}) %reduce-scatter.14.cloned.1.call-update) | async-done | bytes 24592 | tf_op jit(solution)/shard_map/reduce_scatter | solution.py:119
  199.2 0.8 fusion.115
  200.0 8.5 %all_gather.25 = f32[128,192]{1,0:T(8,128)S(1)} all-gather(f32[32,192]{1,0:T(8,128)S(1)} %fusion.115), channel_id=1, replica_groups=mesh['train'=4,'induce'=8] {'train'}, dimensions={0}, use_global_device_ids=true | all-gather | bytes 122880 | tf_op jit(solution)/shard_map/all_gather | solution.py:140
  208.5 0.7 copy.82
  (62 shorter events, 6.1 us)
Async XLA Ops:
  7.2 5.6 %copy-start = (f32[128,192]{0,1:T(8,128)S(1)}, f32[128,192]{0,1:T(8,128)}, u32[]{:S(2)}) copy-start(f32[128,192]{0,1:T(8,128)} %param.6) | copy-start | bytes 294916
  7.2 45.3 %reduce-scatter.10.cloned.1.call-start = ((), (), s32[]{:S(2)}) async-start(), calls=%async_computation.3 | async-start | bytes 163840 | tf_op jit(solution)/shard_map/reduce_scatter | solution.py:119
  12.6 6.4 %copy-start.4 = (f32[64,3,2016]{2,0,1:T(8,128)}, f32[64,3,2016]{2,0,1:T(8,128)S(1)}, u32[]{:S(2)}) copy-start(f32[64,3,2016]{2,0,1:T(8,128)S(1)} %get-tuple-element.27) | copy-start | bytes 4644868
  12.8 6.2 %copy-start.9 = (f32[64,2016]{1,0:T(8,128)}, f32[64,2016]{1,0:T(8,128)S(1)}, u32[]{:S(2)}) copy-start(f32[64,2016]{1,0:T(8,128)S(1)} %multiply_multiply_fusion.1) | copy-start | bytes 1548292
  19.7 41.4 %copy-start.6 = (f32[128,2016]{0,1:T(8,128)}, f32[128,2016]{0,1:T(8,128)S(1)}, u32[]{:S(2)}) copy-start(f32[128,2016]{0,1:T(8,128)S(1)} %get-tuple-element.23) | copy-start | bytes 3096580
  20.4 1.9 copy-start.1
  25.4 93.6 %reduce-scatter.12.cloned.1.call-start = ((), (), s32[]{:S(2)}) async-start(), calls=%async_computation.4 | async-start | bytes 163840 | tf_op jit(solution)/shard_map/reduce_scatter | solution.py:119
  66.4 1.4 copy-start.5
  66.4 1.5 copy-start.10
  84.7 0.6 copy-start.8
  88.1 1.9 copy-start.2
  88.1 2.1 copy-start.7
  94.8 104.4 %reduce-scatter.14.cloned.1.call-start = ((), (), s32[]{:S(2)}) async-start(), calls=%async_computation.5 | async-start | bytes 163840 | tf_op jit(solution)/shard_map/reduce_scatter | solution.py:119
  136.6 1.3 copy-start.11
  156.3 3.7 %copy-start.13 = (f32[32,192]{1,0:T(8,128)S(1)}, f32[32,192]{1,0:T(8,128)}, u32[]{:S(2)}) copy-start(f32[32,192]{1,0:T(8,128)} %get-tuple-element.18) | copy-start | bytes 73732
  170.1 1.9 copy-start.3
  172.0 3.1 %copy-start.15 = (f32[128,192]{0,1:T(8,128)S(1)}, f32[128,192]{0,1:T(8,128)}, u32[]{:S(2)}) copy-start(f32[128,192]{0,1:T(8,128)} %copy.81) | copy-start | bytes 294916
  175.0 24.2 %copy-start.12 = (f32[32,192]{1,0:T(8,128)S(1)}, f32[32,192]{1,0:T(8,128)}, u32[]{:S(2)}) copy-start(f32[32,192]{1,0:T(8,128)} %reduce-scatter.10.cloned.1.call-done) | copy-start | bytes 73732
  175.0 24.2 %copy-start.14 = (f32[32,192]{1,0:T(8,128)S(1)}, f32[32,192]{1,0:T(8,128)}, u32[]{:S(2)}) copy-start(f32[32,192]{1,0:T(8,128)} %reduce-scatter.12.cloned.1.call-done) | copy-start | bytes 73732
Sparse Core Ops, SparseCore 0:
  25.5 26.8 reduce-scatter.9
  94.9 24.0 reduce-scatter.11
  175.1 24.0 reduce-scatter.13
